TPU v7x, 32 devices: a whole 2x2x4 slice. The times are simulated.
32 devices in a mesh: rep: 4 (over x, core), tp: 8 (over z, y).
Axes of the slice: x: 2, y: 2, z: 4, core: 2. Of those that a mesh axis runs over, the one named last changes fastest.
Arguments:
- trainer_query: float32 [32, 256, 8192], P(('rep', 'tp')), may hold values from -6 to 6
- trainer_output: float32 [32, 8192, 256], P(('rep', 'tp')), may hold values from -6 to 6
- probes: bfloat16 [768, 8192], replicated, may hold values from -0.0625 to 0.0625
- shard_block: int32 [32], replicated, may hold values from 0 to 31, each once
- slice_owner: int32 [8], replicated, may hold values from 0 to 7, each once
Outputs:
- query_slices: bfloat16 [8, 8192, 1024], P('tp')
- output_slices: bfloat16 [8, 1024, 8192], P('tp')
- query_prints: float32 [8, 768, 1024], P('tp')
- output_prints: float32 [8, 1024, 768], P('tp')
Inputs may be any that keep to these rules, and one draw needn't show every extreme that they name: `shard_block`: a permutation: each number once. `slice_owner`: a permutation: each number once.
All inputs are finite; a program needn't handle non-finite values.
Results may differ from a plain program's by a relative error of at most 0.0029.
Values may be sent and summed in bfloat16 or wider, within the bound.
A program may use at most 192 MiB of HBM per device.

v0:
```python
import jax
import jax.numpy as jnp
from jax import lax
from jax.sharding import PartitionSpec as P


def per_device(trainer_query, trainer_output, probes, shard_block, slice_owner):
    tp_count = lax.axis_size("tp")
    rep_count = lax.axis_size("rep")
    dev_count = tp_count * rep_count
    shard_rows = trainer_query.shape[1]
    query_width = trainer_query.shape[2]
    slice_width = query_width // tp_count
    model_width = shard_rows * dev_count
    positions = jnp.arange(dev_count, dtype=jnp.int32)
    inverse = jnp.zeros((dev_count,), jnp.int32).at[shard_block].set(positions)
    query_local = trainer_query[0].astype(jnp.bfloat16)
    query_blocks = jnp.take(
        query_local.reshape(shard_rows, tp_count, slice_width), slice_owner, axis=1
    ).reshape(shard_rows, query_width)
    output_local = trainer_output[0].astype(jnp.bfloat16)
    output_blocks = jnp.take(
        output_local.reshape(tp_count, slice_width, shard_rows), slice_owner, axis=0
    ).reshape(query_width, shard_rows)
    query_moved = lax.all_to_all(query_blocks, "tp", split_axis=1, concat_axis=0, tiled=True)
    query_all = lax.all_gather(query_moved, "rep", axis=0, tiled=True)
    output_moved = lax.all_to_all(output_blocks, "tp", split_axis=0, concat_axis=1, tiled=True)
    output_all = lax.all_gather(output_moved, "rep", axis=1, tiled=True)
    query_ordered = query_all.reshape(dev_count, shard_rows, slice_width)
    query_slice = jnp.take(query_ordered, inverse, axis=0).reshape(model_width, slice_width)
    output_ordered = output_all.reshape(slice_width, dev_count, shard_rows)
    output_slice = jnp.take(output_ordered, inverse, axis=1).reshape(slice_width, model_width)
    query_prints = jnp.dot(probes, query_slice, preferred_element_type=jnp.float32)
    output_prints = lax.dot_general(
        output_slice, probes, (((1,), (1,)), ((), ())), preferred_element_type=jnp.float32
    )
    return (query_slice[None], output_slice[None], query_prints[None], output_prints[None])


def solution(mesh):
    placed = (P(("rep", "tp"), None, None), P(("rep", "tp"), None, None), P(), P(), P())
    return jax.shard_map(
        per_device,
        mesh=mesh,
        in_specs=placed,
        out_specs=(
            P("tp", None, None),
            P("tp", None, None),
            P("tp", None, None),
            P("tp", None, None),
        ),
        check_vma=False,
    )
```

profile of v0, /device:TPU:0, one launch (start us, length us, event | category | flops | bytes accessed | tf_op | source)
XLA Modules:
  0.0 447.3 jit_solution(16472503897032174620)
XLA Ops:
  7.2 0.0 all-gather.5.cloned.1.call-start
  7.2 0.7 compare_select_fusion
  7.9 0.7 compare_and_fusion
  8.5 5.8 %convert_element_type.16 = bf16[1,8192,256]{2,1,0:T(8,128)(2,1)} convert(f32[1,8192,256]{2,1,0:T(8,128)} %param.6) | non-fusion elementwise | flops 2097152 | bytes 12582912 | tf_op jit(solution)/shard_map/convert_element_type | solution.py:21
  14.3 5.0 %gather_fusion.2 = bf16[8,1024,256]{2,1,0:T(8,128)(2,1)} fusion(bf16[8,1024,256]{2,1,0:T(8,128)(2,1)} %bitcast.33, s32[1024]{0:T(1024)S(1)} %pad_clamp_fusion.1), kind=kCustom, calls=%fused_computation.2 | custom fusion | bytes 8388640 | tf_op jit(solution)/shard_map/jit(_take)/gather | solution.py:22
  19.4 2.7 broadcast_select_fusion
  22.0 100.4 %all_to_all.32 = bf16[8,1024,256]{2,1,0:T(8,128)(2,1)} all-to-all(bf16[8,1024,256]{2,1,0:T(8,128)(2,1)S(1)} %broadcast_select_fusion), channel_id=1, replica_groups=mesh['rep'=4,'tp'=8] {'tp'}, dimensions={0} | all-to-all | bytes 8388608 | tf_op jit(solution)/shard_map/all_to_all | solution.py:27
  122.4 6.5 %copy.13 = bf16[1024,8,256]{0,2,1:T(8,128)(2,1)} copy(bf16[1024,8,256]{2,0,1:T(8,128)(2,1)} %bitcast.39) | data formatting | bytes 8388608 | tf_op jit(solution)/shard_map/all_to_all | solution.py:27
  128.9 0.0 all-gather.5.cloned.1.call-update
  128.9 0.0 all-gather.3.cloned.1.call-start
  129.0 7.5 %copy.11 = bf16[1,256,8192]{1,2,0:T(8,128)(2,1)} copy(f32[1,256,8192]{2,1,0:T(8,128)} %param.5) | data formatting | bytes 12582912 | tf_op args[0]
  136.5 6.7 %copy.12 = bf16[256,8,1024]{2,0,1:T(8,128)(2,1)} copy(bf16[256,8,1024]{0,2,1:T(8,128)(2,1)} %bitcast.34) | data formatting | bytes 8388608 | tf_op jit(solution)/shard_map/convert_element_type | solution.py:17
  143.2 5.8 %gather_fusion = bf16[8,256,1024]{2,1,0:T(8,128)(2,1)} fusion(bf16[256,8,1024]{2,0,1:T(8,128)(2,1)} %copy.12, s32[1024]{0:T(1024)S(1)} %pad_clamp_fusion.1), kind=kCustom, calls=%fused_computation | custom fusion | bytes 8388640 | tf_op jit(solution)/shard_map/jit(_take)/gather | solution.py:18
  149.0 2.7 select_bitcast_fusion
  151.7 96.2 %all_to_all.33 = bf16[256,8,1024]{2,0,1:T(8,128)(2,1)} all-to-all(bf16[256,8,1024]{2,0,1:T(8,128)(2,1)S(1)} %select_bitcast_fusion), channel_id=1, replica_groups=mesh['rep'=4,'tp'=8] {'tp'}, dimensions={1} | all-to-all | bytes 8388608 | tf_op jit(solution)/shard_map/all_to_all | solution.py:25
  247.9 0.0 all-gather.3.cloned.1.call-update
  248.0 0.0 copy-done
  248.0 0.9 scatter_custom_fusion
  248.9 0.1 broadcast_in_dim.66
  249.0 0.0 all-gather.5.cloned.1.call-done
  249.0 22.8 %copy.14 = bf16[1024,32,256]{2,0,1:T(8,128)(2,1)} copy(bf16[1024,32,256]{0,2,1:T(8,128)(2,1)} %bitcast.35) | data formatting | bytes 33554432 | tf_op jit(solution)/shard_map/reshape | solution.py:31
  271.8 13.4 %gather_fusion.3 = bf16[32,1024,256]{2,1,0:T(8,128)(2,1)} fusion(bf16[1024,32,256]{2,0,1:T(8,128)(2,1)} %copy.14, s32[1024]{0:T(1024)S(1)} %pad_clamp_fusion), kind=kCustom, calls=%fused_computation.3 | custom fusion | bytes 33554560 | tf_op jit(solution)/shard_map/jit(_take)/gather | solution.py:32
  285.2 22.5 %copy.15 = bf16[1024,32,256]{0,2,1:T(8,128)(2,1)} copy(bf16[1024,32,256]{2,0,1:T(8,128)(2,1)} %bitcast.32) | data formatting | bytes 33554432 | tf_op jit(solution)/shard_map/jit(_take)/gather | solution.py:32
  307.6 14.3 %bitcast_select_fusion.2 = bf16[1,1024,8192]{1,2,0:T(8,128)(2,1)} fusion(bf16[1024,32,256]{0,2,1:T(8,128)(2,1)} %copy.15, pred[8192]{0:T(1024)(128)(4,1)S(1)} %broadcast_in_dim.67), kind=kLoop, calls=%fused_computation.7 | loop fusion | flops 8388608 | bytes 33562624 | tf_op jit(solution)/shard_map/jit(_take)/select_n | solution.py:32
  321.9 21.3 %copy.17 = bf16[1,1024,8192]{2,1,0:T(8,128)(2,1)} copy(bf16[1,1024,8192]{1,2,0:T(8,128)(2,1)} %bitcast_select_fusion.2) | data formatting | bytes 33554432
  343.2 14.2 %bitcast_select_fusion = bf16[1024,8192]{0,1:T(8,128)(2,1)} fusion(bf16[1024,32,256]{0,2,1:T(8,128)(2,1)} %copy.15, pred[8192]{0:T(1024)(128)(4,1)S(1)} %broadcast_in_dim.67), kind=kLoop, calls=%fused_computation.5 | loop fusion | flops 8388608 | bytes 33562624 | tf_op jit(solution)/shard_map/jit(_take)/select_n | solution.py:32
  357.3 13.2 %gather_fusion.1 = bf16[32,256,1024]{2,1,0:T(8,128)(2,1)} fusion(bf16[32,256,1024]{2,1,0:T(8,128)(2,1)} %bitcast.36, s32[1024]{0:T(1024)S(1)} %pad_clamp_fusion), kind=kCustom, calls=%fused_computation.1 | custom fusion | bytes 33554560 | tf_op jit(solution)/shard_map/jit(_take)/gather | solution.py:30
  370.6 14.2 %bitcast_select_fusion.1 = bf16[8192,1024]{1,0:T(8,128)(2,1)} fusion(bf16[32,256,1024]{2,1,0:T(8,128)(2,1)} %gather_fusion.1, pred[8192]{0:T(1024)(128)(4,1)S(1)} %broadcast_in_dim.67), kind=kLoop, calls=%fused_computation.6 | loop fusion | flops 8388608 | bytes 33562624 | tf_op jit(solution)/shard_map/jit(_take)/select_n | solution.py:30
  384.7 20.4 %convolution_bitcast_fusion = f32[1,1024,768]{2,1,0:T(8,128)} fusion(bf16[1024,8192]{0,1:T(8,128)(2,1)} %bitcast_select_fusion, bf16[768,8192]{1,0:T(8,128)(2,1)} %param.7), kind=kOutput, calls=%fused_computation.11 | convolution fusion | flops 12884901888 | bytes 32505856 | tf_op jit(solution)/shard_map/dot_general | solution.py:34
  405.1 18.8 %convolution_bitcast_fusion.1 = f32[1,768,1024]{1,2,0:T(8,128)S(1)} fusion(bf16[8192,1024]{1,0:T(8,128)(2,1)} %bitcast_select_fusion.1, bf16[768,8192]{1,0:T(8,128)(2,1)} %param.7), kind=kOutput, calls=%fused_computation.12 | convolution fusion | flops 12884901888 | bytes 32505856 | tf_op jit(solution)/shard_map/dot_general | solution.py:33
  423.9 2.4 copy.18
  426.3 14.2 %bitcast_select_fusion.3 = bf16[1,8192,1024]{2,1,0:T(8,128)(2,1)} fusion(pred[8192]{0:T(1024)(128)(4,1)S(1)} %broadcast_in_dim.67, bf16[1,8192,1024]{2,1,0:T(8,128)(2,1)} %bitcast.31), kind=kLoop, calls=%fused_computation.8 | loop fusion | flops 8388608 | bytes 33562624 | tf_op jit(solution)/shard_map/jit(_take)/select_n | solution.py:30
  (9 shorter events, 0.0 us)
Async XLA Ops:
  7.2 241.8 %all-gather.5.cloned.1.call-start = ((), (), s32[]{:S(2)}) async-start(), calls=%async_computation.3 | async-start | bytes 20971520 | tf_op jit(solution)/shard_map/all_gather | solution.py:28
  128.9 228.4 %all-gather.3.cloned.1.call-start = ((), (), s32[]{:S(2)}) async-start(), calls=%async_computation.2 | async-start | bytes 20971520 | tf_op jit(solution)/shard_map/all_gather | solution.py:26
  149.0 98.9 %copy-start = (s32[32]{0:T(128)S(1)}, s32[32]{0:T(128)}, u32[]{:S(2)}) copy-start(s32[32]{0:T(128)} %param.8) | copy-start | bytes 388
Sparse Core Ops, SparseCore 0:
  129.0 104.8 all-gather.4
  248.1 104.6 all-gather.2
where the time goes:
time: 450 us; the launch traced here: 447 us
  blocking collectives  197 us (44%)
  local copies, waits for them, and re-layouts  128 us (28%)
  other arithmetic  69.3 us (15%)
  matrix products  39.2 us (9%)
  between operations  14.1 us (3%)
    all_to_all x1, blocking collectives, per_device(): lax.all_to_all(output_blocks, 'tp', split_axis=0, concat_axis=1, tiled=True)  100 us
    all_to_all x1, blocking collectives, per_device(): lax.all_to_all(query_blocks, 'tp', split_axis=1, concat_axis=0, tiled=True)  96.2 us
    gather x2, local copies, waits for them, and re-layouts, per_device(): jnp.take(output_ordered, inverse, axis=1).reshape(slice_width, model_width)  35.9 us
    unnamed x5, local copies, waits for them, and re-layouts  31.2 us
    select_n x2, other arithmetic, per_device(): jnp.take(output_ordered, inverse, axis=1).reshape(slice_width, model_width)  28.4 us
    select_n x3, other arithmetic, per_device(): jnp.take(query_ordered, inverse, axis=0).reshape(model_width, slice_width)  28.4 us
    reshape x1, local copies, waits for them, and re-layouts, per_device(): output_ordered = output_all.reshape(slice_width, dev_count, shard_rows)  22.8 us
    dot_general x1, matrix products, per_device(): lax.dot_general(output_slice, probes, (((1,), (1,)), ((), ())), preferred...  20.4 us
  transfers between devices with their start and end apart: 2, of which 0 were waited for; matrix products, arithmetic and copies ran while one was open for 30% of the time, Pallas kernels for 0%

commit v1 on v0

v1 whole, which is shorter than its diff:
```python
import functools

import jax
import jax.numpy as jnp
from jax import lax
from jax.experimental import pallas as pl
from jax.experimental.pallas import tpu as pltpu
from jax.sharding import PartitionSpec as P

MESH = pl.DeviceIdType.MESH


def pack_kernel(owner_ref, query_ref, output_ref, query_blocks, output_blocks):
    query_blocks[...] = query_ref[...].astype(jnp.bfloat16)
    output_blocks[...] = output_ref[...].astype(jnp.bfloat16)


def pack(trainer_query, trainer_output, slice_owner):
    tp_count = slice_owner.shape[0]
    _, rows, width = trainer_query.shape
    cut = width // tp_count
    return pl.pallas_call(
        pack_kernel,
        out_shape=(
            jax.ShapeDtypeStruct((tp_count, rows, cut), jnp.bfloat16),
            jax.ShapeDtypeStruct((tp_count, cut, rows), jnp.bfloat16),
        ),
        grid_spec=pltpu.PrefetchScalarGridSpec(
            num_scalar_prefetch=1,
            grid=(tp_count,),
            in_specs=[
                pl.BlockSpec((1, rows, cut), lambda k, owner: (0, 0, owner[k])),
                pl.BlockSpec((1, cut, rows), lambda k, owner: (0, owner[k], 0)),
            ],
            out_specs=[
                pl.BlockSpec((1, rows, cut), lambda k, owner: (k, 0, 0)),
                pl.BlockSpec((1, cut, rows), lambda k, owner: (k, 0, 0)),
            ],
        ),
    )(slice_owner, trainer_query, trainer_output)


def pair_index(index, offset, count):
    paired, bit = 0, 1
    while bit < count:
        paired = paired + bit * lax.rem(lax.div(index, bit) + (offset // bit) % 2, 2)
        bit *= 2
    return paired


def move_kernel(
    rep_count, tp_count, lag, query_blocks, output_blocks, query_all, output_all,
    swap_send, swap_recv, near_send, near_recv, far_send, far_recv, own_sem,
):
    rep, tp = lax.axis_index("rep"), lax.axis_index("tp")
    partner = rep + 1 - 2 * lax.rem(rep, 2)
    hops = range(1, rep_count // 2)
    ahead = {hop: lax.rem(rep + 2 * hop, rep_count) for hop in hops}
    behind = {hop: lax.rem(rep + rep_count - 2 * hop, rep_count) for hop in hops}
    pairs = [pair_index(tp, offset, tp_count) for offset in range(tp_count)]
    arrays = ((query_blocks, query_all), (output_blocks, output_all))

    barrier = pltpu.get_barrier_semaphore()
    peers = [(rep, pairs[offset]) for offset in range(1, tp_count)]
    peers += [(partner, tp)] + [(ahead[hop], tp) for hop in hops]
    for peer in peers:
        pl.semaphore_signal(barrier, inc=1, device_id=peer, device_id_type=MESH)
    pl.semaphore_wait(barrier, len(peers))

    def send(source, target, send_sem, recv_sem, device):
        copy = pltpu.make_async_remote_copy(
            src_ref=source, dst_ref=target, send_sem=send_sem, recv_sem=recv_sem,
            device_id=device, device_id_type=MESH,
        )
        copy.start()
        return copy

    mine = rep * tp_count + tp
    swaps, nears, fars, owns = {}, {}, {}, []
    for offset in range(1, tp_count):
        for a, (blocks, everything) in enumerate(arrays):
            swaps[offset, a] = send(
                blocks.at[pairs[offset]], everything.at[mine],
                swap_send.at[a, offset], swap_recv.at[a, offset], (rep, pairs[offset]),
            )
    for a, (blocks, everything) in enumerate(arrays):
        own = pltpu.make_async_copy(blocks.at[tp], everything.at[mine], own_sem.at[a])
        own.start()
        owns.append(own)

    def spread(offset, a):
        blocks, everything = arrays[a]
        place = everything.at[rep * tp_count + pairs[offset]]
        if offset:
            swaps[offset, a].wait_recv()
            block = place
        else:
            block = blocks.at[tp]
        for hop in hops:
            fars[hop, offset, a] = send(
                block, place, far_send.at[hop - 1, a, offset], far_recv.at[hop - 1, a, offset],
                (ahead[hop], tp),
            )
        nears[0, offset, a] = send(
            block, place, near_send.at[0, a, offset], near_recv.at[0, a, offset], (partner, tp)
        )

    def relay(offset, a):
        for hop in hops:
            place = arrays[a][1].at[behind[hop] * tp_count + pairs[offset]]
            fars[hop, offset, a].wait_recv()
            nears[hop, offset, a] = send(
                place, place, near_send.at[hop, a, offset], near_recv.at[hop, a, offset],
                (partner, tp),
            )

    units = [(offset, a) for offset in range(tp_count) for a in range(2)]
    for step in range(len(units) + lag):
        if step < len(units):
            spread(*units[step])
        if step >= lag:
            relay(*units[step - lag])
    for copy in nears.values():
        copy.wait_recv()
    for copies in (swaps, fars, nears):
        for copy in copies.values():
            copy.wait_send()
    for own in owns:
        own.wait()


def move(query_blocks, output_blocks, rep_count):
    tp_count = query_blocks.shape[0]
    count = rep_count * tp_count
    half = rep_count // 2
    dma = pltpu.SemaphoreType.DMA
    return pl.pallas_call(
        functools.partial(move_kernel, rep_count, tp_count, 3),
        out_shape=(
            jax.ShapeDtypeStruct((count,) + query_blocks.shape[1:], jnp.bfloat16),
            jax.ShapeDtypeStruct((count,) + output_blocks.shape[1:], jnp.bfloat16),
        ),
        in_specs=[pl.BlockSpec(memory_space=pl.ANY)] * 2,
        out_specs=[pl.BlockSpec(memory_space=pl.ANY)] * 2,
        scratch_shapes=[
            dma((2, tp_count)), dma((2, tp_count)),
            dma((half, 2, tp_count)), dma((half, 2, tp_count)),
            dma((half - 1, 2, tp_count)), dma((half - 1, 2, tp_count)),
            dma((2,)),
        ],
        compiler_params=pltpu.CompilerParams(collective_id=0, has_side_effects=True),
    )(query_blocks, output_blocks)


def query_kernel(group, inverse_ref, *refs):
    blocks, (probes_ref, slice_ref, prints_ref) = refs[:group], refs[group:]
    rows = blocks[0].shape[1]
    for j, block in enumerate(blocks):
        slice_ref[0, j * rows : (j + 1) * rows, :] = block[0]
    part = jnp.dot(probes_ref[...], slice_ref[0], preferred_element_type=jnp.float32)

    @pl.when(pl.program_id(0) == 0)
    def _():
        prints_ref[0] = part

    @pl.when(pl.program_id(0) > 0)
    def _():
        prints_ref[0] += part


def output_kernel(group, inverse_ref, *refs):
    blocks, (probes_ref, slice_ref, prints_ref) = refs[:group], refs[group:]
    rows = blocks[0].shape[2]
    for j, block in enumerate(blocks):
        slice_ref[0, :, j * rows : (j + 1) * rows] = block[0]
    part = lax.dot_general(
        slice_ref[0], probes_ref[...], (((1,), (1,)), ((), ())),
        preferred_element_type=jnp.float32,
    )

    @pl.when(pl.program_id(0) == 0)
    def _():
        prints_ref[0] = part

    @pl.when(pl.program_id(0) > 0)
    def _():
        prints_ref[0] += part


def finish(body, everything, probes, inverse, slice_shape, prints_shape, along):
    count = everything.shape[0]
    block = everything.shape[1:]
    group = max(1, min(count, 1024 // block[along]))
    span = group * block[along]
    tile = list((1,) + block)
    tile[1 + along] = span
    in_specs = [
        pl.BlockSpec((1,) + block, lambda b, inv, j=j: (inv[b * group + j], 0, 0))
        for j in range(group)
    ]
    in_specs.append(pl.BlockSpec((probes.shape[0], span), lambda b, inv: (0, b)))
    place = (lambda b, inv: (0, b, 0)) if along == 0 else (lambda b, inv: (0, 0, b))
    return pl.pallas_call(
        functools.partial(body, group),
        out_shape=(
            jax.ShapeDtypeStruct(slice_shape, jnp.bfloat16),
            jax.ShapeDtypeStruct(prints_shape, jnp.float32),
        ),
        grid_spec=pltpu.PrefetchScalarGridSpec(
            num_scalar_prefetch=1,
            grid=(count // group,),
            in_specs=in_specs,
            out_specs=[
                pl.BlockSpec(tuple(tile), place),
                pl.BlockSpec(prints_shape, lambda b, inv: (0, 0, 0)),
            ],
        ),
    )(inverse, *([everything] * group), probes)


def per_device(trainer_query, trainer_output, probes, shard_block, slice_owner):
    tp_count = lax.axis_size("tp")
    rep_count = lax.axis_size("rep")
    count = tp_count * rep_count
    rows, width = trainer_query.shape[1:]
    cut = width // tp_count
    model = rows * count
    positions = jnp.arange(count, dtype=jnp.int32)
    held = shard_block[None, :] == positions[:, None]
    inverse = jnp.sum(jnp.where(held, positions[None, :], 0), axis=1, dtype=jnp.int32)
    query_blocks, output_blocks = pack(trainer_query, trainer_output, slice_owner)
    query_all, output_all = move(query_blocks, output_blocks, rep_count)
    query_slice, query_prints = finish(
        query_kernel, query_all, probes, inverse,
        (1, model, cut), (1, probes.shape[0], cut), 0,
    )
    output_slice, output_prints = finish(
        output_kernel, output_all, probes, inverse,
        (1, cut, model), (1, cut, probes.shape[0]), 1,
    )
    return query_slice, output_slice, query_prints, output_prints


def solution(mesh):
    placed = (P(("rep", "tp"), None, None), P(("rep", "tp"), None, None), P(), P(), P())
    return jax.shard_map(
        per_device,
        mesh=mesh,
        in_specs=placed,
        out_specs=(
            P("tp", None, None),
            P("tp", None, None),
            P("tp", None, None),
            P("tp", None, None),
        ),
        check_vma=False,
    )
```

time: 450 us -> 266 us (0.59)
  Pallas kernels: 0 us -> 264 us
  blocking collectives: 197 us -> 0 us
  local copies, waits for them, and re-layouts: 128 us -> 0 us
  other arithmetic: 69.3 us -> 1.36 us
  matrix products: 39.2 us -> 0 us
  between operations: 14.1 us -> 0.64 us
    pallas_call x0 -> x4, Pallas kernels: none -> 264 us  [the longest x1 204 us: move(): pl.pallas_call(functools.partial(move_kernel, rep_count, tp_count, 3), ou...]
    all_to_all x2 -> x0, blocking collectives: 197 us -> none  [the longest x1 100 us: per_device(): lax.all_to_all(output_blocks, 'tp', split_axis=0, concat_axis=1, tiled=True)]
    select_n x9 -> x0, other arithmetic: 62.8 us -> none  [the longest x2 28.4 us: per_device(): jnp.take(output_ordered, inverse, axis=1).reshape(slice_width, model_width)]
    gather x5 -> x0, local copies, waits for them, and re-layouts: 59.9 us -> none  [the longest x2 35.9 us: per_device(): jnp.take(output_ordered, inverse, axis=1).reshape(slice_width, model_width)]
    dot_general x2 -> x0, matrix products: 39.2 us -> none  [the longest x1 20.4 us: per_device(): lax.dot_general(output_slice, probes, (((1,), (1,)), ((), ())), preferred...]
    unnamed x5 -> x0, local copies, waits for them, and re-layouts: 31.2 us -> none
    reshape x1 -> x0, local copies, waits for them, and re-layouts: 22.8 us -> none  [per_device(): output_ordered = output_all.reshape(slice_width, dev_count, shard_rows)]
    convert_element_type x1 -> x0, local copies, waits for them, and re-layouts: 6.73 us -> none  [per_device(): query_local = trainer_query[0].astype(jnp.bfloat16)]
  transfers between devices with their start and end apart: 2 -> 0, of which waited for: 0 -> 0; matrix products, arithmetic and copies ran while one was open for 30% -> 0% of each run, Pallas kernels for 0% -> 0%
where the time goes in v1:
time: 266 us
  Pallas kernels  264 us (99%)
    pallas_call x1, Pallas kernels, move(): pl.pallas_call(functools.partial(move_kernel, rep_count, tp_count, 3), ou...  204 us
    pallas_call x2, Pallas kernels, finish(): pl.pallas_call(functools.partial(body, group), out_shape=(jax.ShapeDtypeS...  48.8 us
    pallas_call x1, Pallas kernels, pack(): pl.pallas_call(pack_kernel, out_shape=(jax.ShapeDtypeStruct((tp_count, ro...  11.4 us

profile of v1, /device:TPU:0, one launch (start us, length us, event | category | flops | bytes accessed | tf_op | source)
XLA Modules:
  0.0 266.0 jit_solution(16278763380489254880)
XLA Ops:
  0.6 1.4 select_reduce_fusion.inverse_ref
  2.0 11.4 %shard_map.84 = (bf16[8,256,1024]{2,1,0:T(8,128)(2,1)}, bf16[8,1024,256]{2,1,0:T(8,128)(2,1)}) custom-call(s32[8]{0:T(128)} %owner_ref.1, f32[1,256,8192]{2,1,0:T(8,128)} %query_ref.1, f32[1,8192,256]{2,1,0:T(8,128)} %output_ref.1), custom_call_target="tpu_custom_call" | custom-call | tf_op jit(solution)/shard_map/pallas_call | solution.py:22
  13.4 203.7 %shard_map.85 = (bf16[32,256,1024]{2,1,0:T(8,128)(2,1)}, bf16[32,1024,256]{2,1,0:T(8,128)(2,1)}) custom-call(bf16[8,256,1024]{2,1,0:T(8,128)(2,1)} %get-tuple-element.12.query_blocks, bf16[8,1024,256]{2,1,0:T(8,128)(2,1)} %get-tuple-element.13.output_blocks), custom_call_target="tpu_custom_call" | custom-call | tf_op jit(solution)/shard_map/pallas_call | solution.py:137
  217.1 24.3 %shard_map.86 = (bf16[1,8192,1024]{2,1,0:T(8,128)(2,1)}, f32[1,768,1024]{2,1,0:T(8,128)}) custom-call(s32[32]{0:T(128)} %select_reduce_fusion.inverse_ref, bf16[32,256,1024]{2,1,0:T(8,128)(2,1)} %get-tuple-element.14.refs_0_.refs_1_.refs_2_.refs_3_, bf16[32,256,1024]{2,1,0:T(8,128)(2,1)} %get-tuple-element.14.refs_0_.refs_1_.refs_2_.refs_3_, ...), custom_call_target="tpu_custom_call" | custom-call | tf_op jit(solution)/shard_map/pallas_call | solution.py:203
  241.5 24.5 %shard_map.87 = (bf16[1,1024,8192]{2,1,0:T(8,128)(2,1)}, f32[1,1024,768]{2,1,0:T(8,128)}) custom-call(s32[32]{0:T(128)} %select_reduce_fusion.inverse_ref, bf16[32,1024,256]{2,1,0:T(8,128)(2,1)} %get-tuple-element.16.refs_0_.refs_1_.refs_2_.refs_3_, bf16[32,1024,256]{2,1,0:T(8,128)(2,1)} %get-tuple-element.16.refs_0_.refs_1_.refs_2_.refs_3_, ...), custom_call_target="tpu_custom_call" | custom-call | tf_op jit(solution)/shard_map/pallas_call | solution.py:203

commit v2 on v1

--- a/solution.py
+++ b/solution.py
@@ -43,113 +43,271 @@
 def pair_index(index, offset, count):
     paired, bit = 0, 1
     while bit < count:
-        paired = paired + bit * lax.rem(lax.div(index, bit) + (offset // bit) % 2, 2)
+        low = lax.rem(lax.div(index, bit) + lax.div(offset, bit), 2)
+        paired = paired + bit * low
         bit *= 2
     return paired
 
 
-def move_kernel(
-    rep_count, tp_count, lag, query_blocks, output_blocks, query_all, output_all,
-    swap_send, swap_recv, near_send, near_recv, far_send, far_recv, own_sem,
-):
+def move_kernel(rep_count, tp_count, multiply, *refs):
+    if multiply:
+        (owner_ref, query_blocks, output_blocks, probes_ref,
+         query_all, output_all, query_prints, output_prints,
+         swap_send, swap_recv, near_send, near_recv, far_send, far_recv, own_sem,
+         probes, picked, query_tile, output_tile, load_sem, probes_sem) = refs
+    else:
+        (query_blocks, output_blocks, query_all, output_all,
+         swap_send, swap_recv, near_send, near_recv, far_send, far_recv, own_sem) = refs
     rep, tp = lax.axis_index("rep"), lax.axis_index("tp")
     partner = rep + 1 - 2 * lax.rem(rep, 2)
     hops = range(1, rep_count // 2)
     ahead = {hop: lax.rem(rep + 2 * hop, rep_count) for hop in hops}
     behind = {hop: lax.rem(rep + rep_count - 2 * hop, rep_count) for hop in hops}
-    pairs = [pair_index(tp, offset, tp_count) for offset in range(tp_count)]
+    across = {hop: lax.rem(partner + rep_count - 2 * hop, rep_count) for hop in hops}
     arrays = ((query_blocks, query_all), (output_blocks, output_all))
+    mine = rep * tp_count + tp
+    count = rep_count * tp_count
+    rows = query_blocks.shape[1]
+
+    def load_probes(block):
+        columns = pl.ds(pl.multiple_of(block * rows, rows), rows)
+        return pltpu.make_async_copy(
+            probes_ref.at[:, columns], probes.at[block], probes_sem.at[block]
+        )
+
+    def pair(offset):
+        return pair_index(tp, jnp.int32(offset), tp_count)
 
     barrier = pltpu.get_barrier_semaphore()
-    peers = [(rep, pairs[offset]) for offset in range(1, tp_count)]
+    peers = [(rep, pair(offset)) for offset in range(1, tp_count)]
     peers += [(partner, tp)] + [(ahead[hop], tp) for hop in hops]
     for peer in peers:
         pl.semaphore_signal(barrier, inc=1, device_id=peer, device_id_type=MESH)
     pl.semaphore_wait(barrier, len(peers))
 
-    def send(source, target, send_sem, recv_sem, device):
-        copy = pltpu.make_async_remote_copy(
+    def remote(source, target, send_sem, recv_sem, device):
+        return pltpu.make_async_remote_copy(
             src_ref=source, dst_ref=target, send_sem=send_sem, recv_sem=recv_sem,
             device_id=device, device_id_type=MESH,
         )
-        copy.start()
-        return copy
-
-    mine = rep * tp_count + tp
-    swaps, nears, fars, owns = {}, {}, {}, []
-    for offset in range(1, tp_count):
-        for a, (blocks, everything) in enumerate(arrays):
-            swaps[offset, a] = send(
-                blocks.at[pairs[offset]], everything.at[mine],
-                swap_send.at[a, offset], swap_recv.at[a, offset], (rep, pairs[offset]),
-            )
-    for a, (blocks, everything) in enumerate(arrays):
-        own = pltpu.make_async_copy(blocks.at[tp], everything.at[mine], own_sem.at[a])
-        own.start()
-        owns.append(own)
-
-    def spread(offset, a):
+
+    def swap(offset, a):
         blocks, everything = arrays[a]
-        place = everything.at[rep * tp_count + pairs[offset]]
-        if offset:
-            swaps[offset, a].wait_recv()
-            block = place
-        else:
-            block = blocks.at[tp]
+        return remote(
+            blocks.at[pair(offset)], everything.at[mine],
+            swap_send.at[a, offset], swap_recv.at[a, offset], (rep, pair(offset)),
+        )
+
+    def far(hop, offset, a, block, place):
+        return remote(
+            block, place, far_send.at[hop - 1, a, offset], far_recv.at[hop - 1, a, offset],
+            (ahead[hop], tp),
+        )
+
+    def near(hop, offset, a, block, place):
+        return remote(
+            block, place, near_send.at[hop, a, offset], near_recv.at[hop, a, offset],
+            (partner, tp),
+        )
+
+    def place_of(group, offset, a):
+        return arrays[a][1].at[group * tp_count + pair(offset)]
+
+    def own(a):
+        blocks, everything = arrays[a]
+        return pltpu.make_async_copy(blocks.at[tp], everything.at[mine], own_sem.at[a])
+
+    def spread(offset, a, block):
+        place = place_of(rep, offset, a)
         for hop in hops:
-            fars[hop, offset, a] = send(
-                block, place, far_send.at[hop - 1, a, offset], far_recv.at[hop - 1, a, offset],
-                (ahead[hop], tp),
-            )
-        nears[0, offset, a] = send(
-            block, place, near_send.at[0, a, offset], near_recv.at[0, a, offset], (partner, tp)
-        )
+            far(hop, offset, a, block, place).start()
+        near(0, offset, a, block, place).start()
 
     def relay(offset, a):
         for hop in hops:
-            place = arrays[a][1].at[behind[hop] * tp_count + pairs[offset]]
-            fars[hop, offset, a].wait_recv()
-            nears[hop, offset, a] = send(
-                place, place, near_send.at[hop, a, offset], near_recv.at[hop, a, offset],
-                (partner, tp),
+            place = place_of(behind[hop], offset, a)
+            far(hop, offset, a, place, place).wait_recv()
+            near(hop, offset, a, place, place).start()
+
+    def collect(offset, a):
+        for hop in (0, *hops):
+            place = place_of(rep, offset, a)
+            near(hop, offset, a, place, place).wait_recv()
+
+        @pl.when(offset == 0)
+        def _():
+            own(a).wait()
+            if multiply and a == 0:
+
+                @pl.loop(0, count)
+                def _(block):
+                    load_probes(block).wait()
+
+
+        if not multiply:
+            return
+        groups = [rep, partner]
+        for hop in hops:
+            groups += [behind[hop], across[hop]]
+        tile, prints = ((query_tile, query_prints), (output_tile, output_prints))[a]
+        loads = []
+        for j, group in enumerate(groups):
+            spot = (pl.ds(j * rows, rows), slice(None))
+            load = pltpu.make_async_copy(
+                place_of(group, offset, a), tile.at[spot if a == 0 else spot[::-1]],
+                load_sem.at[a, j],
             )
-
-    units = [(offset, a) for offset in range(tp_count) for a in range(2)]
-    for step in range(len(units) + lag):
-        if step < len(units):
-            spread(*units[step])
-        if step >= lag:
-            relay(*units[step - lag])
-    for copy in nears.values():
-        copy.wait_recv()
-    for copies in (swaps, fars, nears):
-        for copy in copies.values():
-            copy.wait_send()
-    for own in owns:
-        own.wait()
-
-
-def move(query_blocks, output_blocks, rep_count):
-    tp_count = query_blocks.shape[0]
+            load.start()
+            loads.append(load)
+        for j, group in enumerate(groups):
+            owner = owner_ref[group * tp_count + pair(offset)]
+            picked[:, j * rows : (j + 1) * rows] = probes[owner]
+        for load in loads:
+            load.wait()
+        if a == 0:
+            prints[0] += jnp.dot(picked[...], tile[...], preferred_element_type=jnp.float32)
+        else:
+            prints[0] += lax.dot_general(
+                tile[...], picked[...], (((1,), (1,)), ((), ())),
+                preferred_element_type=jnp.float32,
+            )
+
+    for offset in range(1, tp_count):
+        for a in range(2):
+            swap(offset, a).start()
+    for a in range(2):
+        spread(jnp.int32(0), a, arrays[a][0].at[tp])
+    for a in range(2):
+        own(a).start()
+    if multiply:
+
+        @pl.loop(0, count)
+        def _(block):
+            load_probes(block).start()
+
+        query_prints[...] = jnp.zeros_like(query_prints)
+        output_prints[...] = jnp.zeros_like(output_prints)
+
+    @pl.loop(1, tp_count + 2)
+    def _(step):
+        for a in range(2):
+
+            @pl.when(step < tp_count)
+            def _():
+                swap(step, a).wait_recv()
+                spread(step, a, place_of(rep, step, a))
+
+            @pl.when(step <= tp_count)
+            def _():
+                relay(step - 1, a)
+
+            if a == 0:
+
+                @pl.when(step >= 2)
+                def _():
+                    collect(step - 2, 1)
+
+            else:
+
+                @pl.when(step <= tp_count)
+                def _():
+                    collect(step - 1, 0)
+
+    @pl.loop(0, tp_count)
+    def _(offset):
+        for a in range(2):
+
+            @pl.when(offset > 0)
+            def _():
+                swap(offset, a).wait_send()
+
+            place = place_of(rep, offset, a)
+            for hop in hops:
+                far(hop, offset, a, place, place).wait_send()
+            for hop in (0, *hops):
+                near(hop, offset, a, place, place).wait_send()
+
+
+def move(query_blocks, output_blocks, probes, shard_block, rep_count, multiply):
+    tp_count, rows, cut = query_blocks.shape
     count = rep_count * tp_count
     half = rep_count // 2
+    kinds = probes.shape[0]
     dma = pltpu.SemaphoreType.DMA
+    anywhere = pl.BlockSpec(memory_space=pl.ANY)
+    shapes = [
+        jax.ShapeDtypeStruct((count, rows, cut), jnp.bfloat16),
+        jax.ShapeDtypeStruct((count, cut, rows), jnp.bfloat16),
+    ]
+    scratch = [
+        dma((2, tp_count)), dma((2, tp_count)),
+        dma((half, 2, tp_count)), dma((half, 2, tp_count)),
+        dma((half - 1, 2, tp_count)), dma((half - 1, 2, tp_count)),
+        dma((2,)),
+    ]
+    operands, in_specs, out_specs = [query_blocks, output_blocks], [anywhere] * 2, [anywhere] * 2
+    if multiply:
+        operands = [shard_block] + operands + [probes]
+        in_specs = [pl.BlockSpec(memory_space=pltpu.SMEM)] + [anywhere] * 3
+        out_specs += [pl.BlockSpec(memory_space=pltpu.VMEM)] * 2
+        shapes += [
+            jax.ShapeDtypeStruct((1, kinds, cut), jnp.float32),
+            jax.ShapeDtypeStruct((1, cut, kinds), jnp.float32),
+        ]
+        scratch += [
+            pltpu.VMEM((count, kinds, rows), jnp.bfloat16),
+            pltpu.VMEM((kinds, rep_count * rows), jnp.bfloat16),
+            pltpu.VMEM((rep_count * rows, cut), jnp.bfloat16),
+            pltpu.VMEM((cut, rep_count * rows), jnp.bfloat16),
+            dma((2, rep_count)),
+            dma((count,)),
+        ]
     return pl.pallas_call(
-        functools.partial(move_kernel, rep_count, tp_count, 3),
+        functools.partial(move_kernel, rep_count, tp_count, multiply),
+        out_shape=shapes,
+        in_specs=in_specs,
+        out_specs=out_specs,
+        scratch_shapes=scratch,
+        compiler_params=pltpu.CompilerParams(collective_id=0, has_side_effects=True),
+    )(*operands)
+
+
+def order_kernel(group, inverse_ref, *refs):
+    queries, outputs = refs[:group], refs[group : 2 * group]
+    query_slice, output_slice = refs[2 * group :]
+    rows = queries[0].shape[1]
+    for j in range(group):
+        query_slice[0, j * rows : (j + 1) * rows, :] = queries[j][0]
+        output_slice[0, :, j * rows : (j + 1) * rows] = outputs[j][0]
+
+
+def order(query_all, output_all, inverse):
+    count, rows, cut = query_all.shape
+    group = max(1, min(count, 1024 // rows))
+    picks = range(group)
+    return pl.pallas_call(
+        functools.partial(order_kernel, group),
         out_shape=(
-            jax.ShapeDtypeStruct((count,) + query_blocks.shape[1:], jnp.bfloat16),
-            jax.ShapeDtypeStruct((count,) + output_blocks.shape[1:], jnp.bfloat16),
-        ),
-        in_specs=[pl.BlockSpec(memory_space=pl.ANY)] * 2,
-        out_specs=[pl.BlockSpec(memory_space=pl.ANY)] * 2,
-        scratch_shapes=[
-            dma((2, tp_count)), dma((2, tp_count)),
-            dma((half, 2, tp_count)), dma((half, 2, tp_count)),
-            dma((half - 1, 2, tp_count)), dma((half - 1, 2, tp_count)),
-            dma((2,)),
-        ],
-        compiler_params=pltpu.CompilerParams(collective_id=0, has_side_effects=True),
-    )(query_blocks, output_blocks)
+            jax.ShapeDtypeStruct((1, count * rows, cut), jnp.bfloat16),
+            jax.ShapeDtypeStruct((1, cut, count * rows), jnp.bfloat16),
+        ),
+        grid_spec=pltpu.PrefetchScalarGridSpec(
+            num_scalar_prefetch=1,
+            grid=(count // group,),
+            in_specs=[
+                pl.BlockSpec((1, rows, cut), lambda b, inv, j=j: (inv[b * group + j], 0, 0))
+                for j in picks
+            ]
+            + [
+                pl.BlockSpec((1, cut, rows), lambda b, inv, j=j: (inv[b * group + j], 0, 0))
+                for j in picks
+            ],
+            out_specs=[
+                pl.BlockSpec((1, group * rows, cut), lambda b, inv: (0, b, 0)),
+                pl.BlockSpec((1, cut, group * rows), lambda b, inv: (0, 0, b)),
+            ],
+        ),
+    )(inverse, *([query_all] * group), *([output_all] * group))
 
 
 def query_kernel(group, inverse_ref, *refs):
@@ -229,7 +387,13 @@
     held = shard_block[None, :] == positions[:, None]
     inverse = jnp.sum(jnp.where(held, positions[None, :], 0), axis=1, dtype=jnp.int32)
     query_blocks, output_blocks = pack(trainer_query, trainer_output, slice_owner)
-    query_all, output_all = move(query_blocks, output_blocks, rep_count)
+    multiply = rows % 128 == 0
+    moved = move(query_blocks, output_blocks, probes, shard_block, rep_count, multiply)
+    if multiply:
+        query_all, output_all, query_prints, output_prints = moved
+        query_slice, output_slice = order(query_all, output_all, inverse)
+        return query_slice, output_slice, query_prints, output_prints
+    query_all, output_all = moved
     query_slice, query_prints = finish(
         query_kernel, query_all, probes, inverse,
         (1, model, cut), (1, probes.shape[0], cut), 0,

time: 266 us -> 255 us (0.959)
  Pallas kernels: 264 us -> 248 us
  local copies, waits for them, and re-layouts: 0 us -> 4.68 us
    pallas_call x3 -> x2, Pallas kernels: 253 us -> 236 us  [the longest x1 212 us: move(): pl.pallas_call(functools.partial(move_kernel, rep_count, tp_count, multip...]
    unnamed x0 -> x6, local copies, waits for them, and re-layouts: none -> 4.68 us
where the time goes in v2:
time: 255 us; the launch traced here: 254 us
  Pallas kernels  248 us (97%)
  local copies, waits for them, and re-layouts  4.68 us (2%)
    pallas_call x1, Pallas kernels, move(): pl.pallas_call(functools.partial(move_kernel, rep_count, tp_count, multip...  212 us
    pallas_call x1, Pallas kernels, order(): pl.pallas_call(functools.partial(order_kernel, group), out_shape=(jax.Sha...  23.8 us
    pallas_call x1, Pallas kernels, pack(): pl.pallas_call(pack_kernel, out_shape=(jax.ShapeDtypeStruct((tp_count, ro...  11.4 us

profile of v2, /device:TPU:0, one launch (start us, length us, event | category | flops | bytes accessed | tf_op | source)
XLA Modules:
  0.0 254.2 jit_solution(7599716230293266581)
XLA Ops:
  0.6 1.3 select_reduce_fusion.inverse_ref
  1.9 11.4 %shard_map.84 = (bf16[8,256,1024]{2,1,0:T(8,128)(2,1)}, bf16[8,1024,256]{2,1,0:T(8,128)(2,1)}) custom-call(s32[8]{0:T(128)} %owner_ref.1, f32[1,256,8192]{2,1,0:T(8,128)} %query_ref.1, f32[1,8192,256]{2,1,0:T(8,128)} %output_ref.1), custom_call_target="tpu_custom_call" | custom-call | tf_op jit(solution)/shard_map/pallas_call | solution.py:22
  13.4 212.4 %shard_map.85 = (bf16[32,256,1024]{2,1,0:T(8,128)(2,1)}, bf16[32,1024,256]{2,1,0:T(8,128)(2,1)}, f32[1,768,1024]{2,1,0:T(8,128)}, f32[1,1024,768]{2,1,0:T(8,128)}) custom-call(s32[32]{0:T(128)} %refs_0_.1, bf16[8,256,1024]{2,1,0:T(8,128)(2,1)} %get-tuple-element.12.refs_1_, bf16[8,1024,256]{2,1,0:T(8,128)(2,1)} %get-tuple-element.13.refs_2_, ...), custom_call_target="tpu_custom_call" | custom-call | tf_op jit(solution)/shard_map/pallas_call | solution.py:265
  225.7 0.0 copy-start.1
  225.7 23.8 %shard_map.86 = (bf16[1,8192,1024]{2,1,0:T(8,128)(2,1)}, bf16[1,1024,8192]{2,1,0:T(8,128)(2,1)}) custom-call(s32[32]{0:T(128)} %select_reduce_fusion.inverse_ref, bf16[32,256,1024]{2,1,0:T(8,128)(2,1)} %get-tuple-element.14.refs_0_.refs_1_.refs_2_.refs_3_, bf16[32,256,1024]{2,1,0:T(8,128)(2,1)} %get-tuple-element.14.refs_0_.refs_1_.refs_2_.refs_3_, ...), custom_call_target="tpu_custom_call" | custom-call | tf_op jit(solution)/shard_map/pallas_call | solution.py:288
  249.5 0.0 copy-start
  249.5 0.0 copy-done.1
  249.5 1.7 copy.11
  251.2 1.3 copy-done
  252.5 1.7 copy.12
Async XLA Ops:
  225.7 23.8 %copy-start.1 = (f32[1,768,1024]{2,1,0:T(8,128)S(1)}, f32[1,768,1024]{2,1,0:T(8,128)}, u32[]{:S(2)}) copy-start(f32[1,768,1024]{2,1,0:T(8,128)} %get-tuple-element.26) | copy-start | bytes 9437188
  249.5 3.0 %copy-start = (f32[1,1024,768]{2,1,0:T(8,128)S(1)}, f32[1,1024,768]{2,1,0:T(8,128)}, u32[]{:S(2)}) copy-start(f32[1,1024,768]{2,1,0:T(8,128)} %get-tuple-element.27) | copy-start | bytes 9437188
